TPU v7x, 128 devices: a whole 4x4x4 slice. The times are simulated.
128 devices in a mesh: rep: 2 (over core), dp: 64 (over x, y, z).
Axes of the slice: x: 4, y: 4, z: 4, core: 2. Of those that a mesh axis runs over, the one named last changes fastest.
Arguments:
- g_w_gate: bfloat16 [128, 2, 1024, 3200], P(('rep', 'dp')), parts along dimension 0
- g_w_up: bfloat16 [128, 2, 1024, 3200], P(('rep', 'dp')), parts along dimension 0
- g_w_down: bfloat16 [128, 2, 3200, 1024], P(('rep', 'dp')), parts along dimension 0
- w_gate: bfloat16 [2, 1024, 3200], replicated
- w_up: bfloat16 [2, 1024, 3200], replicated
- w_down: bfloat16 [2, 3200, 1024], replicated
- m_w_gate: float32 [2, 1024, 3200], P(None, 'dp')
- m_w_up: float32 [2, 1024, 3200], P(None, 'dp')
- m_w_down: float32 [2, 3200, 1024], P(None, 'dp')
- v_w_gate: float32 [2, 1024, 3200], P(None, 'dp')
- v_w_up: float32 [2, 1024, 3200], P(None, 'dp')
- v_w_down: float32 [2, 3200, 1024], P(None, 'dp')
Outputs:
- output 1: bfloat16 [4, 1024, 3200], P('rep'), parts along dimension 0
- output 2: bfloat16 [4, 1024, 3200], P('rep'), parts along dimension 0
- output 3: bfloat16 [4, 3200, 1024], P('rep'), parts along dimension 0
- output 4: float32 [4, 1024, 3200], P('rep', 'dp'), parts along dimension 0
- output 5: float32 [4, 1024, 3200], P('rep', 'dp'), parts along dimension 0
- output 6: float32 [4, 3200, 1024], P('rep', 'dp'), parts along dimension 0
- output 7: float32 [4, 1024, 3200], P('rep', 'dp'), parts along dimension 0
- output 8: float32 [4, 1024, 3200], P('rep', 'dp'), parts along dimension 0
- output 9: float32 [4, 3200, 1024], P('rep', 'dp'), parts along dimension 0
There are 2 independent parts. A program takes and returns all parts, laid end to end along the dimension named above; an argument that names none is the same for every part.
All inputs are finite; a program needn't handle non-finite values.
Results may differ from a plain program's by a relative error of at most 0.022.
Values are sent between devices in bfloat16 or wider.
A program may use at most 1.5 GiB of HBM per device.

v0:
```python
import jax
import jax.numpy as jnp
from jax import lax
from jax.sharding import PartitionSpec as P


def adamw(w, m, v, g):
    m = 0.9 * m + 0.1 * g
    v = 0.95 * v + 0.05 * g * g
    step = m * lax.rsqrt(v + 1e-8) + 0.1 * w
    return (w - 0.02 * step).astype(jnp.bfloat16), m, v


def solution(mesh):
    def step(*arrays):
        terms, weights, m, v = (arrays[i : i + 3] for i in (0, 3, 6, 9))
        gradients = [lax.psum_scatter(t[0], "dp", scatter_dimension=1, tiled=True).astype(jnp.float32) for t in terms]
        me = lax.axis_index("dp")
        own = [lax.dynamic_slice_in_dim(w, me * one.shape[1], one.shape[1], 1).astype(jnp.float32) for w, one in zip(weights, m, strict=True)]
        new = [adamw(w, m, v, g) for w, m, v, g in zip(own, m, v, gradients, strict=True)]
        whole = [lax.all_gather(one[0], "dp", axis=1, tiled=True) for one in new]
        return (*whole, *(one[1] for one in new), *(one[2] for one in new))

    all_of, cut = P(None, None, None), P(None, "dp", None)
    return jax.shard_map(
        step,
        mesh=mesh,
        in_specs=(P(("rep", "dp"), None, None, None),) * 3 + (all_of,) * 3 + (cut,) * 6,
        out_specs=(P("rep", None, None),) * 3 + (P("rep", "dp", None),) * 6,
        check_vma=False,
    )
```

profile of v0, /device:TPU:0, one launch (start us, length us, event | category | flops | bytes accessed | tf_op | source)
XLA Modules:
  0.0 1296.9 jit_solution(17770700589144017621)
XLA Ops:
  7.2 0.0 all-reduce.3.cloned.1.call-start
  7.2 24.6 %copy.30 = bf16[1,2,3200,1024]{3,1,2,0:T(2,128)(2,1)} copy(bf16[1,2,3200,1024]{3,2,1,0:T(8,128)(2,1)} %param.14) | data formatting | bytes 26214400 | tf_op args[2]
  31.8 0.0 reduce-scatter.5.cloned.1.call-start
  32.0 0.6 reduce-scatter.5.cloned.1.call-update
  32.6 0.0 reduce-scatter.3.cloned.1.call-start
  32.6 0.7 reduce-scatter.3.cloned.1.call-update
  33.3 0.0 all-gather.8.cloned.1.call-start
  33.4 0.6 dynamic-slice
  34.6 1.0 constant_dynamic-slice_fusion
  35.6 188.6 %all-reduce.3.cloned.1.call-done = bf16[2,3200,1024]{2,0,1:T(2,128)(2,1)} async-done(((bf16[2,3200,1024]{2,0,1:T(2,128)(2,1)}), bf16[2,3200,1024]{2,0,1:T(2,128)(2,1)}) %all-reduce.3.cloned.1.call-update) | async-done | bytes 13107216
  224.2 2.9 fusion.14
  227.2 0.0 all-gather.6.cloned.1.call-start
  227.2 379.4 %reduce-scatter.5.cloned.1.call-done = bf16[2,16,3200]{2,1,0:T(8,128)(2,1)} async-done(((bf16[2,1024,3200]{2,1,0:T(8,128)(2,1)}), bf16[2,16,3200]{2,1,0:T(8,128)(2,1)}) %reduce-scatter.5.cloned.1.call-update) | async-done | bytes 204816 | tf_op jit(solution)/shard_map/reduce_scatter | solution.py:17
  606.6 2.1 fusion.6
  608.7 0.0 all-gather.4.cloned.1.call-start
  608.8 380.2 %reduce-scatter.3.cloned.1.call-done = bf16[2,16,3200]{2,1,0:T(8,128)(2,1)} async-done(((bf16[2,1024,3200]{2,1,0:T(8,128)(2,1)}), bf16[2,16,3200]{2,1,0:T(8,128)(2,1)}) %reduce-scatter.3.cloned.1.call-update) | async-done | bytes 204816 | tf_op jit(solution)/shard_map/reduce_scatter | solution.py:17
  988.9 2.1 fusion.2
  991.0 88.5 %all-gather.8.cloned.1.call-done = bf16[2,3200,1024]{2,0,1:T(2,128)(2,1)} async-done(((bf16[2,50,1024]{2,0,1:T(2,128)(2,1)}), bf16[2,3200,1024]{2,0,1:T(2,128)(2,1)}) %all-gather.8.cloned.1.call-update) | async-done | bytes 13107216 | tf_op jit(solution)/shard_map/all_gather | solution.py:21
  1079.6 12.9 copy.26
  1092.5 83.1 %all-gather.6.cloned.1.call-done = bf16[2,1024,3200]{2,1,0:T(8,128)(2,1)} async-done(((bf16[2,16,3200]{2,1,0:T(8,128)(2,1)}), bf16[2,1024,3200]{2,1,0:T(8,128)(2,1)}) %all-gather.6.cloned.1.call-update) | async-done | bytes 13107216 | tf_op jit(solution)/shard_map/all_gather | solution.py:21
  1175.6 96.1 %all-gather.4.cloned.1.call-done = bf16[2,1024,3200]{2,1,0:T(8,128)(2,1)} async-done(((bf16[2,16,3200]{2,1,0:T(8,128)(2,1)}), bf16[2,1024,3200]{2,1,0:T(8,128)(2,1)}) %all-gather.4.cloned.1.call-update) | async-done | bytes 13107216 | tf_op jit(solution)/shard_map/all_gather | solution.py:21
  1271.7 11.4 copy.34
  1283.0 2.0 copy-done
  1285.1 4.9 copy.35
  (19 shorter events, 0.1 us)
Async XLA Ops:
  7.2 217.0 %all-reduce.3.cloned.1.call-start = ((), (), s32[]{:S(2)}) async-start(), calls=%async_computation.7 | async-start | bytes 26214400
  31.8 574.8 %reduce-scatter.5.cloned.1.call-start = ((), (), s32[]{:S(2)}) async-start(), calls=%async_computation.4 | async-start | bytes 13312000 | tf_op jit(solution)/shard_map/reduce_scatter | solution.py:17
  31.9 1.5 copy-start.7
  31.9 192.3 %copy-start.1 = (f32[2,50,1024]{2,0,1:T(2,128)S(1)}, f32[2,50,1024]{2,0,1:T(2,128)}, u32[]{:S(2)}) copy-start(f32[2,50,1024]{2,0,1:T(2,128)} %param.23) | copy-start | bytes 1228804
  31.9 192.3 %copy-start.2 = (f32[2,50,1024]{2,0,1:T(2,128)S(1)}, f32[2,50,1024]{2,0,1:T(2,128)}, u32[]{:S(2)}) copy-start(f32[2,50,1024]{2,0,1:T(2,128)} %param.20) | copy-start | bytes 1228804
  31.9 574.7 %copy-start.3 = (f32[2,16,3200]{2,1,0:T(8,128)S(1)}, f32[2,16,3200]{2,1,0:T(8,128)}, u32[]{:S(2)}) copy-start(f32[2,16,3200]{2,1,0:T(8,128)} %param.22) | copy-start | bytes 1228804
  31.9 574.7 %copy-start.4 = (f32[2,16,3200]{2,1,0:T(8,128)S(1)}, f32[2,16,3200]{2,1,0:T(8,128)}, u32[]{:S(2)}) copy-start(f32[2,16,3200]{2,1,0:T(8,128)} %param.19) | copy-start | bytes 1228804
  31.9 957.0 %copy-start.5 = (f32[2,16,3200]{2,1,0:T(8,128)S(1)}, f32[2,16,3200]{2,1,0:T(8,128)}, u32[]{:S(2)}) copy-start(f32[2,16,3200]{2,1,0:T(8,128)} %param.21) | copy-start | bytes 1228804
  32.0 957.0 %copy-start.6 = (f32[2,16,3200]{2,1,0:T(8,128)S(1)}, f32[2,16,3200]{2,1,0:T(8,128)}, u32[]{:S(2)}) copy-start(f32[2,16,3200]{2,1,0:T(8,128)} %param.18) | copy-start | bytes 1228804
  32.6 956.3 %reduce-scatter.3.cloned.1.call-start = ((), (), s32[]{:S(2)}) async-start(), calls=%async_computation.2 | async-start | bytes 13312000 | tf_op jit(solution)/shard_map/reduce_scatter | solution.py:17
  33.3 1046.2 %all-gather.8.cloned.1.call-start = ((), (), s32[]{:S(2)}) async-start(), calls=%async_computation.6 | async-start | bytes 13312000 | tf_op jit(solution)/shard_map/all_gather | solution.py:21
  227.2 948.4 %all-gather.6.cloned.1.call-start = ((), (), s32[]{:S(2)}) async-start(), calls=%async_computation.5 | async-start | bytes 13312000 | tf_op jit(solution)/shard_map/all_gather | solution.py:21
  608.7 663.0 %all-gather.4.cloned.1.call-start = ((), (), s32[]{:S(2)}) async-start(), calls=%async_computation.3 | async-start | bytes 13312000 | tf_op jit(solution)/shard_map/all_gather | solution.py:21
  1271.7 13.4 %copy-start = (bf16[2,1024,3200]{2,1,0:T(8,128)(2,1)S(1)}, bf16[2,1024,3200]{2,1,0:T(8,128)(2,1)}, u32[]{:S(2)}) copy-start(bf16[2,1024,3200]{2,1,0:T(8,128)(2,1)} %all-gather.6.cloned.1.call-done) | copy-start | bytes 39321604
Sparse Core Ops, SparseCore 0:
  31.9 192.2 all-reduce.2
  226.6 379.9 reduce-scatter.4
  609.0 379.8 reduce-scatter.2
  992.2 87.2 all-gather.7
  1082.9 92.6 all-gather.5
  1178.9 92.6 all-gather.3
where the time goes:
time: 1300 us
  waiting for transfers between devices  1220 us (94%)
  local copies, waits for them, and re-layouts  57.5 us (4%)
  between operations  14.9 us (1%)
    reduce_scatter x2, waiting for transfers between devices, step(): lax.psum_scatter(t[0], 'dp', scatter_dimension=1, tiled=True)  760 us
    all_gather x3, waiting for transfers between devices, step(): whole = [lax.all_gather(one[0], 'dp', axis=1, tiled=True) for one in new]  268 us
    unnamed x7, waiting for transfers between devices  190 us
    unnamed x21, local copies, waits for them, and re-layouts  56.5 us
  transfers between devices with their start and end apart: 6, of which 6 were waited for; matrix products, arithmetic and copies ran while one was open for 2% of the time, Pallas kernels for 0%

commit v1 on v0

v1 whole, which is shorter than its diff:
```python
import functools

import jax
import jax.numpy as jnp
from jax import lax
from jax.experimental import pallas as pl
from jax.experimental.pallas import tpu as pltpu
from jax.sharding import PartitionSpec as P

F32, BF16 = jnp.float32, jnp.bfloat16
MESH = pl.DeviceIdType.MESH
STAGES = 12


class Part:
    def __init__(self, order, chunks, width, units, window, step, rows):
        self.order, self.chunks, self.width = order, chunks, width
        self.units, self.window, self.step, self.rows = units, window, step, rows
        self.down = window > 1


PARTS = (
    Part("yzx", 5, 640, 4, 1, 1, 16),
    Part("zxy", 5, 640, 4, 1, 1, 16),
    Part("xyz", 4, 256, 25, 7, 6, 8),
)
SCRATCH = ("G", "CB", "SA", "LA", "RA", "SB", "LB", "RB", "SC", "LC", "RC", "XC", "GO", "WN", "M", "mb", "vb", "wb", "send", "recv", "gsend", "grecv", "loc", "pre")


def scratch(p):
    k, u, w, r, n = p.chunks, p.units, p.width, p.rows, p.window
    slab = lambda *lead: pltpu.VMEM((*lead, 4, u, r, w), BF16)
    group = lambda *lead: pltpu.VMEM((*lead, u, r, w), BF16)
    win = lambda *lead: pltpu.VMEM((*lead, n, r, w), BF16)
    dma = pltpu.SemaphoreType.DMA
    return {
        "G": slab(k, 2), "CB": slab(2, 2), "SA": slab(k, 2), "LA": slab(k, 2), "RA": slab(k, 2),
        "SB": group(k, 2), "LB": group(k, 2), "RB": group(k, 2),
        "SC": win(k, 2), "LC": win(k, 2), "RC": win(k, 2), "XC": win(k, 4), "GO": win(k, 2),
        "WN": win(k, 4, 2) if p.down else win(k, 2),
        "M": group(k, 2) if p.down else pltpu.VMEM((8, 128), BF16),
        "mb": pltpu.VMEM((2, n, r, k * w), F32), "vb": pltpu.VMEM((2, n, r, k * w), F32), "wb": pltpu.VMEM((2, n, r, k * w), BF16),
        "send": dma((k, 3, 6)), "recv": dma((k, 3, 6)), "gsend": dma((k, 3, 4)), "grecv": dma((k, 3, 4)),
        "loc": dma((k, 5)), "pre": dma((3,)),
    }


class Later:
    def __init__(self, describe):
        self.describe = describe

    def start(self):
        self.describe().start()

    def wait(self):
        self.describe().wait()

    def wait_send(self):
        self.describe().wait_send()

    def wait_recv(self):
        self.describe().wait_recv()


class Run:
    def __init__(self, p, at, g, w, m, v, out, gout, **buffers):
        self.p, self.gh, self.wh, self.mh, self.vh, self.out, self.gout = p, g, w, m, v, out, gout
        self.at = at
        self.me = tuple(at[axis] for axis in p.order)
        self.__dict__.update(buffers)

    def device(self, phase, offset):
        to = dict(self.at)
        axis = self.p.order[phase]
        to[axis] = lax.rem(to[axis] + offset, 4)
        return {"dp": to["x"] * 16 + to["y"] * 4 + to["z"]}

    def near(self, phase, offset):
        return lax.rem(self.me[phase] + offset, 4)

    def cols(self, c):
        return pl.ds(pl.multiple_of(c * self.p.width, 128), self.p.width)

    def hbm(self, ref, layer, c, a=None, b=None, z=None):
        of = dict(zip(self.p.order, (a, b, z)))
        full = lambda axis: slice(None) if of[axis] is None else of[axis]
        if self.p.down:
            return ref.at[layer, full("x"), full("y"), :, :, self.cols(c)]
        return ref.at[layer, full("x"), full("y"), full("z"), :, self.cols(c)]

    def slab(self, ref, k, i, b):
        return ref.at[k, i, :, b] if self.p.order == "yzx" else ref.at[k, i, b]

    def unit(self, ref, k, i, b, j):
        return ref.at[k, i, j, b] if self.p.order == "yzx" else ref.at[k, i, b, j]

    def window(self, ref, k, i, z):
        return ref.at[k, i, pl.ds(z * self.p.step, self.p.window)]

    def to(self, src, dst, sems, phase, kind, c, offset):
        send, recv = sems
        return Later(
            lambda: pltpu.make_async_remote_copy(
                src_ref=src, dst_ref=dst, send_sem=send.at[c, phase, kind], recv_sem=recv.at[c, phase, kind],
                device_id=self.device(phase, offset), device_id_type=MESH,
            )
        )

    def rs(self, src, dst, phase, kind, c):
        return self.to(src, dst, (self.send, self.recv), phase, kind, c, 1 if kind % 2 == 0 else 3)

    def ag(self, src, dst, phase, kind, c):
        return self.to(src, dst, (self.gsend, self.grecv), phase, kind, c, 1 if kind % 2 == 0 else 3)

    def add(self, n, dst, *srcs):
        @pl.loop(0, n)
        def _(j):
            total = srcs[0](j)[...].astype(F32)
            for s in srcs[1:]:
                total = total + s(j)[...].astype(F32)
            dst(j)[...] = total.astype(BF16)

    def sum_copies(self, phase, c):
        rows = (self.SA, self.SB, self.SC)[phase], (self.LA, self.LB, self.LC)[phase], (self.RA, self.RB, self.RC)[phase]
        s, l, r = rows
        right, left, opposite = self.near(phase, 1), self.near(phase, 3), self.near(phase, 2)
        if phase == 0:
            src = [self.hbm(self.gh, i, c, a=a) for i, a in ((0, opposite), (1, opposite), (1, right), (0, left))]
        elif phase == 1:
            src = [self.slab(self.LA, c, i, b) for i, b in ((0, opposite), (1, opposite), (1, right), (0, left))]
        else:
            src = [self.XC.at[c, i] for i in range(4)]
        src += [s.at[c, 0], s.at[c, 1]]
        if phase == 0:
            src[4:] = [self.SA.at[c, 0], self.SA.at[c, 1]]
        dst = [s.at[c, 0], s.at[c, 1], l.at[c, 1], r.at[c, 0], l.at[c, 0], r.at[c, 1]]
        return [self.rs(src[kind], dst[kind], phase, kind, c) for kind in range(6)]

    def gather_place(self, phase, layer, c, offset):
        a, b, z = self.me
        if phase == 2:
            z = self.near(2, offset)
            return self.WN.at[c, z, layer] if self.p.down else self.hbm(self.out, layer, c, a, b, z)
        if phase == 1:
            return self.hbm(self.out, layer, c, a, self.near(1, offset))
        return self.hbm(self.out, layer, c, self.near(0, offset))

    def gather_copies(self, phase, c):
        both = pl.ds(0, 2)
        mine = self.gather_place(phase, both, c, 0)
        src = mine
        if phase == 2 and not self.p.down:
            src = self.WN.at[c, :, 0]
        if phase == 1 and self.p.down:
            src = self.M.at[c]
        first = self.gather_place(phase, 0, c, 3)
        second = self.gather_place(phase, 1, c, 1)
        return [
            self.ag(src, mine, phase, 0, c), self.ag(src, mine, phase, 1, c),
            self.ag(first, first, phase, 2, c), self.ag(second, second, phase, 3, c),
        ]

    def gather_arrivals(self, phase, c):
        both = pl.ds(0, 2)
        places = [(both, 3), (both, 1), (0, 2), (1, 2)]
        refs = [self.gather_place(phase, layer, c, offset) for layer, offset in places]
        return [self.ag(ref, ref, phase, kind, c) for kind, ref in enumerate(refs)]

    def local(self, c):
        a = self.me[0]
        b, z = self.me[1:]
        both = pl.ds(0, 2)
        copy = lambda *refs: Later(lambda: pltpu.make_async_copy(*refs))
        half = lax.rem(c, 2)
        if self.p.down:
            new = copy(self.M.at[c], self.hbm(self.out, both, c, a, b), self.loc.at[c, 3])
        else:
            new = copy(self.WN.at[c, :, 0], self.hbm(self.out, both, c, a, b, z), self.loc.at[c, 3])
        return [
            copy(self.hbm(self.gh, 0, c, a=self.near(0, 1)), self.CB.at[half, 0], self.loc.at[c, 0]),
            copy(self.hbm(self.gh, 1, c, a=self.near(0, 3)), self.CB.at[half, 1], self.loc.at[c, 1]),
            copy(self.hbm(self.gh, both, c, a=a), self.G.at[c], self.loc.at[c, 2]),
            new,
            copy(self.GO.at[c], self.gout.at[:, :, :, self.cols(c)], self.loc.at[c, 4]),
        ]

    def preload(self):
        a = self.at
        if self.p.down:
            w = self.wh.at[:, a["x"], a["y"], pl.ds(a["z"] * self.p.step, self.p.window)]
            dst = self.wb
        else:
            w, dst = self.wh.at[:, a["x"], a["y"], a["z"]], self.wb.at[:, 0]
        return [
            pltpu.make_async_copy(self.mh, self.mb, self.pre.at[0]),
            pltpu.make_async_copy(self.vh, self.vb, self.pre.at[1]),
            pltpu.make_async_copy(w, dst, self.pre.at[2]),
        ]

    def kept(self, c, i, b, j):
        return [lambda u, ref=ref: self.unit(ref, c, i, b, j(u)) for ref in (self.G, self.LA, self.RA)]

    def stage(self, s, c):
        p = self.p
        if s == 0:
            copies, local = self.sum_copies(0, c), self.local(c)
            for kind in (0, 1, 2, 3):
                copies[kind].start()
            for one in local[:3]:
                one.start()
        elif s == 1:
            copies, local = self.sum_copies(0, c), self.local(c)
            half = lax.rem(c, 2)
            for h in (0, 1):
                local[h].wait()
                copies[h].wait_recv()
                at = lambda ref, k: (lambda u: ref.at[k, h, lax.div(u, p.units), lax.rem(u, p.units)])
                self.add(4 * p.units, at(self.SA, c), at(self.SA, c), at(self.CB, half))
                copies[4 + h].start()
        elif s == 2:
            before, copies = self.sum_copies(0, c), self.sum_copies(1, c)
            for kind in (2, 3, 4, 5):
                before[kind].wait_recv()
            self.local(c)[2].wait()
            right, left, opposite = self.near(1, 1), self.near(1, 3), self.near(1, 2)
            for kind, (i, b) in enumerate(((0, opposite), (1, opposite), (1, right), (0, left))):
                srcs = self.kept(c, i, b, lambda u: u)
                self.add(p.units, srcs[1], *srcs)
                copies[kind].start()
        elif s == 3:
            copies = self.sum_copies(1, c)
            for h, b in ((0, self.near(1, 1)), (1, self.near(1, 3))):
                copies[h].wait_recv()
                dst = lambda u: self.SB.at[c, h, u]
                self.add(p.units, dst, *self.kept(c, h, b, lambda u: u), dst)
                copies[4 + h].start()
        elif s == 4:
            before, copies = self.sum_copies(1, c), self.sum_copies(2, c)
            for kind in (2, 3, 4, 5):
                before[kind].wait_recv()
            right, left, opposite = self.near(2, 1), self.near(2, 3), self.near(2, 2)
            for kind, (i, z) in enumerate(((0, opposite), (1, opposite), (1, right), (0, left))):
                self.add(p.window, lambda u: self.XC.at[c, kind, u], *self.own_sum(c, i, z))
                copies[kind].start()
        elif s == 5:
            copies = self.sum_copies(2, c)
            for h, z in ((0, self.near(2, 1)), (1, self.near(2, 3))):
                copies[h].wait_recv()
                dst = lambda u: self.SC.at[c, h, u]
                self.add(p.window, dst, *self.own_sum(c, h, z), dst)
                copies[4 + h].start()
        elif s == 6:
            before, copies, local = self.sum_copies(2, c), self.gather_copies(2, c), self.local(c)
            for kind in (2, 3, 4, 5):
                before[kind].wait_recv()

            @pl.when(c == 0)
            def _():
                for one in self.preload():
                    one.wait()

            self.update(c)
            copies[0].start()
            copies[1].start()
            local[4].start()
            if not p.down:
                local[3].start()
        elif s in (7, 9, 11):
            phase = {7: 2, 9: 1, 11: 0}[s]
            arrivals, copies = self.gather_arrivals(phase, c), self.gather_copies(phase, c)
            arrivals[0].wait_recv()
            copies[2].start()
            arrivals[1].wait_recv()
            copies[3].start()
        elif s == 8:
            arrivals, copies = self.gather_arrivals(2, c), self.gather_copies(1, c)
            arrivals[2].wait_recv()
            arrivals[3].wait_recv()
            if p.down:
                self.merge(c)
                self.local(c)[3].start()
            else:
                self.local(c)[3].wait()
            copies[0].start()
            copies[1].start()
        elif s == 10:
            arrivals, copies = self.gather_arrivals(1, c), self.gather_copies(0, c)
            arrivals[2].wait_recv()
            arrivals[3].wait_recv()
            if p.down:
                self.local(c)[3].wait()
            copies[0].start()
            copies[1].start()

    def own_sum(self, c, i, z):
        first = z * self.p.step
        place = lambda u: first + u
        srcs = self.kept(c, i, self.me[1], place)
        return [*srcs, *(lambda u, ref=ref: ref.at[c, i, place(u)] for ref in (self.LB, self.RB))]

    def update(self, c):
        p = self.p
        cols = self.cols(c)
        z = self.me[2]
        for i in (0, 1):
            srcs = [*self.own_sum(c, i, z), lambda u, i=i: self.LC.at[c, i, u], lambda u, i=i: self.RC.at[c, i, u]]

            @pl.loop(0, p.window)
            def _(u):
                total = srcs[0](u)[...].astype(F32)
                for s in srcs[1:]:
                    total = total + s(u)[...].astype(F32)
                g = total.astype(BF16)
                self.GO[c, i, u] = g
                g = g.astype(F32)
                m = 0.9 * self.mb[i, u, :, cols] + 0.1 * g
                v = 0.95 * self.vb[i, u, :, cols] + 0.05 * g * g
                w = self.wb[i, u, :, cols].astype(F32)
                w = (w - 0.02 * (m * lax.rsqrt(v + 1e-8) + 0.1 * w)).astype(BF16)
                if p.down:
                    self.WN[c, z, i, u] = w
                else:
                    self.WN[c, i, u] = w

    def merge(self, c):
        p = self.p
        row = lax.broadcasted_iota(jnp.int32, (p.rows, p.width), 0)
        for i in (0, 1):
            for z in range(4):
                low = 0 if z == 0 else 1
                high = 7 if z == 3 else 6

                @pl.loop(low, high)
                def _(u):
                    self.M[c, i, 6 * z + u] = self.WN[c, z, i, u]

                if z:
                    below = self.WN[c, z - 1, i, 6].astype(F32)
                    above = self.WN[c, z, i, 0].astype(F32)
                    self.M[c, i, 6 * z] = jnp.where(row < 2 * z, below, above).astype(BF16)

    def finish(self, c):
        for arrival in self.gather_arrivals(0, c)[2:]:
            arrival.wait_recv()
        for phase in range(3):
            for copy in (*self.sum_copies(phase, c), *self.gather_copies(phase, c)):
                copy.wait_send()
        self.local(c)[4].wait()


def kernel(*refs):
    ins, outs, rest = refs[:12], refs[12:18], refs[18:]
    i = lax.axis_index("dp")
    at = {"x": lax.div(i, 16), "y": lax.rem(lax.div(i, 4), 4), "z": lax.rem(i, 4)}
    runs = []
    for n, p in enumerate(PARTS):
        buffers = dict(zip(SCRATCH, rest[n * len(SCRATCH) : (n + 1) * len(SCRATCH)]))
        runs.append(Run(p, at, *(ins[n + 3 * which] for which in range(4)), outs[n], outs[n + 3], **buffers))
    last = max(p.chunks for p in PARTS) + STAGES - 1

    barrier = pltpu.get_barrier_semaphore()
    for phase in range(3):
        for offset in (1, 3):
            pl.semaphore_signal(barrier, inc=1, device_id=runs[0].device(phase, offset), device_id_type=MESH)
    pl.semaphore_wait(barrier, 6)
    for run in runs:
        for one in run.preload():
            one.start()

    @pl.loop(0, last)
    def _(t):
        for s in range(STAGES):
            for run in runs:

                @pl.when((t >= s) & (t - s < run.p.chunks))
                def _(run=run, s=s):
                    run.stage(s, t - s)

    for run in runs:

        @pl.loop(0, run.p.chunks)
        def _(c, run=run):
            run.finish(c)


def sum_step_gather(terms, weights, m, v):
    shapes = [(2, 4, 4, 4, 16, 3200)] * 2 + [(2, 4, 4, 25, 8, 1024)]
    own = [(2, 1, 16, 3200)] * 2 + [(2, 7, 8, 1024)]
    args = [a.reshape(s) for group, ss in ((terms, shapes), (weights, shapes), (m, own), (v, own)) for a, s in zip(group, ss, strict=True)]
    held = [one for p in PARTS for one in (lambda made: [made[name] for name in SCRATCH])(scratch(p))]
    hbm = pl.BlockSpec(memory_space=pl.ANY)
    return pl.pallas_call(
        kernel,
        name="sum_step_gather",
        out_shape=[jax.ShapeDtypeStruct(s, BF16) for s in (*shapes, *own)],
        in_specs=[hbm] * 12,
        out_specs=[hbm] * 6,
        scratch_shapes=held,
        compiler_params=pltpu.CompilerParams(collective_id=0, has_side_effects=True, vmem_limit_bytes=67_043_328),
    )(*args)


def solution(mesh):
    def step(*arrays):
        terms, weights, m, v = (arrays[i : i + 3] for i in (0, 3, 6, 9))
        z = lax.rem(lax.axis_index("dp"), 4)
        widen = lambda a: lax.dynamic_update_slice(jnp.zeros((2, 56, 1024), F32), a, (0, 2 * z, 0))
        out = sum_step_gather(terms, weights, [*m[:2], widen(m[2])], [*v[:2], widen(v[2])])
        new = [a.reshape(w.shape) for a, w in zip(out[:3], weights, strict=True)]
        g = [out[3].reshape(2, 16, 3200), out[4].reshape(2, 16, 3200)]
        g.append(lax.dynamic_slice(out[5].reshape(2, 56, 1024), (0, 2 * z, 0), (2, 50, 1024)))
        g = [a.astype(F32) for a in g]
        new_m = [0.9 * a + 0.1 * b for a, b in zip(m, g, strict=True)]
        new_v = [0.95 * a + 0.05 * b * b for a, b in zip(v, g, strict=True)]
        return (*new, *new_m, *new_v)

    all_of, cut = P(None, None, None), P(None, "dp", None)
    return jax.shard_map(
        step,
        mesh=mesh,
        in_specs=(P(("rep", "dp"), None, None, None),) * 3 + (all_of,) * 3 + (cut,) * 6,
        out_specs=(P("rep", None, None),) * 3 + (P("rep", "dp", None),) * 6,
        check_vma=False,
    )
```

time: 1300 us -> 335 us (0.26)
  waiting for transfers between devices: 1220 us -> 0 us
  Pallas kernels: 0 us -> 296 us
  local copies, waits for them, and re-layouts: 57.5 us -> 32.4 us
  between operations: 14.9 us -> 0.74 us
    reduce_scatter x2 -> x0, waiting for transfers between devices: 760 us -> none  [step(): lax.psum_scatter(t[0], 'dp', scatter_dimension=1, tiled=True)]
    pallas_call x0 -> x1, Pallas kernels: none -> 296 us  [sum_step_gather(): pl.pallas_call(kernel, name='sum_step_gather', out_shape=[jax.ShapeDtypeS...]
    all_gather x3 -> x0, waiting for transfers between devices: 268 us -> none  [step(): whole = [lax.all_gather(one[0], 'dp', axis=1, tiled=True) for one in new]]
    unnamed x7 -> x0, waiting for transfers between devices: 190 us -> none
    unnamed x21 -> x19, local copies, waits for them, and re-layouts: 56.5 us -> 30.5 us
  transfers between devices with their start and end apart: 6 -> 0, of which waited for: 6 -> 0; matrix products, arithmetic and copies ran while one was open for 2% -> 0% of each run, Pallas kernels for 0% -> 0%
where the time goes in v1:
time: 335 us
  Pallas kernels  296 us (88%)
  local copies, waits for them, and re-layouts  32.4 us (10%)
  other arithmetic  5.56 us (2%)
    pallas_call x1, Pallas kernels, sum_step_gather(): pl.pallas_call(kernel, name='sum_step_gather', out_shape=[jax.ShapeDtypeS...  296 us
    unnamed x19, local copies, waits for them, and re-layouts  30.5 us

profile of v1, /device:TPU:0, one launch (start us, length us, event | category | flops | bytes accessed | tf_op | source)
XLA Modules:
  0.0 335.2 jit_solution(3263925153619483698)
XLA Ops:
  0.6 1.1 copy.21
  1.8 0.4 dynamic_update_slice.6
  2.2 0.0 copy-start.2
  2.3 0.8 copy-done.2
  3.0 1.1 copy.22
  4.2 0.4 dynamic_update_slice.7
  4.6 0.0 copy-start.1
  4.6 0.8 copy-done.1
  5.4 296.5 %sum_step_gather.1 = (bf16[2,4,4,4,16,3200]{5,4,3,2,1,0:T(8,128)(2,1)}, bf16[2,4,4,4,16,3200]{5,4,3,2,1,0:T(8,128)(2,1)}, bf16[2,4,4,25,8,1024]{5,4,3,2,1,0:T(8,...) custom-call(bf16[2,4,4,4,16,3200]{5,4,3,2,1,0:T(8,128)(2,1)} %bitcast, ...), custom_call_target="tpu_custom_call" | custom-call | tf_op jit(solution)/shard_map/sum_step_gather/pallas_call | solution.py:392
  301.9 2.8 fusion.3
  304.7 1.0 constant_dynamic-slice_fusion
  305.7 2.7 fusion.1
  308.4 0.0 copy-start
  308.4 0.0 slice-start
  308.5 0.0 slice-start.1
  308.5 0.0 slice-start.2
  308.5 12.7 %copy.33 = bf16[2,1024,3200]{2,1,0:T(8,128)(2,1)} copy(bf16[2,1024,3200]{2,1,0:T(8,128)(2,1)} %bitcast.30) | data formatting | bytes 26214400
  321.2 0.0 copy-done
  321.2 6.6 %copy.34 = bf16[2,1024,3200]{2,1,0:T(8,128)(2,1)} copy(bf16[2,1024,3200]{2,1,0:T(8,128)(2,1)S(1)} %bitcast.29) | data formatting | bytes 26214400
  327.8 0.0 slice-done
  327.8 1.2 slice-done.1
  329.0 1.2 slice-done.2
  330.2 0.1 slice-done.3
  330.3 4.9 %copy.35 = bf16[2,3200,1024]{2,1,0:T(8,128)(2,1)} copy(bf16[2,3200,1024]{2,1,0:T(8,128)(2,1)S(1)} %bitcast.28) | data formatting | bytes 26214400
  (4 shorter events, 0.1 us)
Async XLA Ops:
  2.2 0.8 copy-start.2
  4.6 0.8 copy-start.1
  308.4 12.7 %copy-start = (bf16[2,4,4,4,16,3200]{5,4,3,2,1,0:T(8,128)(2,1)S(1)}, bf16[2,4,4,4,16,3200]{5,4,3,2,1,0:T(8,128)(2,1)}, u32[]{:S(2)}) copy-start(bf16[2,4,4,4,16,3200]{5,4,3,2,1,0:T(8,128)(2,1)} %get-tuple-element.16) | copy-start | bytes 39321604
  308.4 19.4 %slice-start = ((s8[13107200]{0:T(1024)(128)(4,1)}), s8[4194304]{0:T(1024)(128)(4,1)S(1)}, s32[]{:S(2)}) async-start(s8[13107200]{0:T(1024)(128)(4,1)} %bitcast.26), calls=%async_computation | async-start | bytes 8388608
  308.5 20.5 %slice-start.1 = ((s8[13107200]{0:T(1024)(128)(4,1)}), s8[4194304]{0:T(1024)(128)(4,1)S(1)}, s32[]{:S(2)}) async-start(s8[13107200]{0:T(1024)(128)(4,1)} %bitcast.26), calls=%async_computation.1 | async-start | bytes 8388608
  308.5 21.7 %slice-start.2 = ((s8[13107200]{0:T(1024)(128)(4,1)}), s8[4194304]{0:T(1024)(128)(4,1)S(1)}, s32[]{:S(2)}) async-start(s8[13107200]{0:T(1024)(128)(4,1)} %bitcast.26), calls=%async_computation.2 | async-start | bytes 8388608
  321.2 9.1 %slice-start.3 = ((s8[13107200]{0:T(1024)(128)(4,1)}), s8[524288]{0:T(1024)(128)(4,1)S(1)}, s32[]{:S(2)}) async-start(s8[13107200]{0:T(1024)(128)(4,1)} %bitcast.26), calls=%async_computation.3 | async-start | bytes 1048576

commit v2 on v1

v2 whole, which is shorter than its diff:
```python
import functools

import jax
import jax.numpy as jnp
from jax import lax
from jax.experimental import pallas as pl
from jax.experimental.pallas import tpu as pltpu
from jax.sharding import PartitionSpec as P

F32, BF16 = jnp.float32, jnp.bfloat16
MESH = pl.DeviceIdType.MESH
STAGES = 12
VMEM_LIMIT = 24 << 20


class Part:
    def __init__(self, order, chunks, width, units, window, step, rows):
        self.order, self.chunks, self.width = order, chunks, width
        self.units, self.window, self.step, self.rows = units, window, step, rows
        self.down = window > 1


PARTS = (
    Part("yzx", 5, 640, 4, 1, 1, 16),
    Part("zxy", 5, 640, 4, 1, 1, 16),
    Part("xyz", 4, 256, 25, 7, 6, 8),
)
SCRATCH = ("CB", "SB", "LB", "RB", "SC", "LC", "RC", "XC", "WN", "mb", "vb", "wb", "send", "recv", "gsend", "grecv", "loc", "pre", "free")


def scratch(p):
    k, u, w, r, n = p.chunks, p.units, p.width, p.rows, p.window
    group = lambda *lead: pltpu.VMEM((*lead, u, r, w), BF16)
    win = lambda *lead: pltpu.VMEM((*lead, n, r, w), BF16)
    moment = pltpu.VMEM((2, n * r, k * w) if p.down else (8, 128), F32)
    dma = pltpu.SemaphoreType.DMA
    return {
        "CB": group(2, 2, 4), "SB": group(k, 2), "LB": group(k, 2), "RB": group(k, 2),
        "SC": win(k, 2), "LC": win(k, 2), "RC": win(k, 2), "XC": win(k, 4),
        "WN": win(k, 4, 2) if p.down else pltpu.VMEM((16, 128), BF16),
        "mb": moment, "vb": moment, "wb": pltpu.VMEM((2, n, r, k * w), BF16),
        "send": dma((k, 3, 6)), "recv": dma((k, 3, 6)), "gsend": dma((k, 3, 4)), "grecv": dma((k, 3, 4)),
        "loc": dma((k, 3)), "pre": dma((3,)), "free": pltpu.SemaphoreType.REGULAR((k, 3)),
    }


class Later:
    def __init__(self, describe):
        self.describe = describe

    def start(self):
        self.describe().start()

    def wait(self):
        self.describe().wait()

    def wait_send(self):
        self.describe().wait_send()

    def wait_recv(self):
        self.describe().wait_recv()


class Run:
    def __init__(self, p, at, g, w, m, v, out, mout, vout, **buffers):
        self.p, self.gh, self.wh, self.mh, self.vh = p, g, w, m, v
        self.out, self.mout, self.vout = out, mout, vout
        self.at = at
        self.me = tuple(at[axis] for axis in p.order)
        self.__dict__.update(buffers)

    def device(self, phase, offset):
        to = dict(self.at)
        axis = self.p.order[phase]
        to[axis] = lax.rem(to[axis] + offset, 4)
        return {"dp": to["x"] * 16 + to["y"] * 4 + to["z"]}

    def near(self, phase, offset):
        return lax.rem(self.me[phase] + offset, 4)

    def cols(self, c):
        return pl.ds(pl.multiple_of(c * self.p.width, 128), self.p.width)

    def part(self, ref, layer, c, a=None, b=None, z=None):
        of = dict(zip(self.p.order, (a, b, z)))
        full = lambda axis: slice(None) if of[axis] is None else of[axis]
        if self.p.down:
            units = slice(None) if z is None else z
            return ref.at[layer, full("x"), full("y"), units, :, self.cols(c)]
        return ref.at[layer, full("x"), full("y"), full("z"), :, self.cols(c)]

    def raw(self, i, q, first, second, c):
        where = {"yzx": (first, q, second), "zxy": (first, second, q), "xyz": (q, first, second)}[self.p.order]
        return self.out.at[(i, *where, slice(None), self.cols(c))]

    def to(self, src, dst, sems, phase, kind, c):
        send, recv = sems
        offset = 1 if kind % 2 == 0 else 3
        return Later(
            lambda: pltpu.make_async_remote_copy(
                src_ref=src, dst_ref=dst, send_sem=send.at[c, phase, kind], recv_sem=recv.at[c, phase, kind],
                device_id=self.device(phase, offset), device_id_type=MESH,
            )
        )

    def credit(self, phase, c):
        for offset in (1, 3):
            pl.semaphore_signal(self.free.at[c, phase], inc=1, device_id=self.device(phase, offset), device_id_type=MESH)

    def add(self, n, dst, *srcs):
        @pl.loop(0, n)
        def _(j):
            total = srcs[0](j)[...].astype(F32)
            for s in srcs[1:]:
                total = total + s(j)[...].astype(F32)
            dst(j)[...] = total.astype(BF16)

    def sum_copies(self, phase, c):
        right, left, opposite = self.near(phase, 1), self.near(phase, 3), self.near(phase, 2)
        kinds = ((0, opposite), (1, opposite), (1, right), (0, left))
        if phase == 0:
            mine = self.me[0]
            at = lambda i, a: self.part(self.out, i, c, a)
            src = [self.part(self.gh, i, c, a) for i, a in kinds] + [at(0, opposite), at(1, opposite)]
            dst = [at(0, left), at(1, right), at(1, mine), at(0, mine), at(0, mine), at(1, mine)]
        else:
            s, l, r = ((self.SB, self.LB, self.RB), (self.SC, self.LC, self.RC))[phase - 1]
            if phase == 1:
                src = [self.part(self.out, i, c, self.near(0, 3), b) for i, b in kinds]
            else:
                src = [self.XC.at[c, i] for i in range(4)]
            src += [s.at[c, 0], s.at[c, 1]]
            dst = [s.at[c, 0], s.at[c, 1], l.at[c, 1], r.at[c, 0], l.at[c, 0], r.at[c, 1]]
        return [self.to(src[kind], dst[kind], (self.send, self.recv), phase, kind, c) for kind in range(6)]

    def sum_arrivals(self, phase, c):
        if phase:
            return self.sum_copies(phase, c)
        right, left, opposite = self.near(0, 1), self.near(0, 3), self.near(0, 2)
        places = ((0, opposite), (1, opposite), (1, left), (0, right), (0, left), (1, right))
        refs = [self.part(self.out, i, c, a) for i, a in places]
        return [self.to(ref, ref, (self.send, self.recv), 0, kind, c) for kind, ref in enumerate(refs)]

    def gather_place(self, phase, layer, c, offset):
        a, b, z = self.me
        if phase == 2:
            z = self.near(2, offset)
            return self.WN.at[c, z, layer] if self.p.down else self.part(self.out, layer, c, a, b, z)
        if phase == 1:
            return self.part(self.out, layer, c, a, self.near(1, offset))
        return self.part(self.out, layer, c, self.near(0, offset))

    def gather_copies(self, phase, c):
        mine = self.gather_place(phase, pl.ds(0, 2), c, 0)
        first = self.gather_place(phase, 0, c, 3)
        second = self.gather_place(phase, 1, c, 1)
        sems = (self.gsend, self.grecv)
        return [self.to(ref, ref, sems, phase, kind, c) for kind, ref in enumerate((mine, mine, first, second))]

    def gather_arrivals(self, phase, c):
        both = pl.ds(0, 2)
        places = [(both, 3), (both, 1), (0, 2), (1, 2)]
        refs = [self.gather_place(phase, layer, c, offset) for layer, offset in places]
        return [self.to(ref, ref, (self.gsend, self.grecv), phase, kind, c) for kind, ref in enumerate(refs)]

    def local(self, c):
        copy = lambda *refs: Later(lambda: pltpu.make_async_copy(*refs))
        half, mine, both = lax.rem(c, 2), self.me[0], pl.ds(0, 2)
        return [
            copy(self.part(self.gh, 0, c, self.near(0, 1)), self.CB.at[half, 0], self.loc.at[c, 0]),
            copy(self.part(self.gh, 1, c, self.near(0, 3)), self.CB.at[half, 1], self.loc.at[c, 1]),
            copy(self.part(self.gh, both, c, mine), self.part(self.out, both, c, mine), self.loc.at[c, 2]),
        ]

    def preload(self):
        a = self.at
        if self.p.down:
            w = self.wh.at[:, a["x"], a["y"], pl.ds(a["z"] * self.p.step, self.p.window)]
            dst = self.wb
        else:
            w, dst = self.wh.at[:, a["x"], a["y"], a["z"]], self.wb.at[:, 0]
        return [
            pltpu.make_async_copy(self.mh, self.mout, self.pre.at[0]),
            pltpu.make_async_copy(self.vh, self.vout, self.pre.at[1]),
            pltpu.make_async_copy(w, dst, self.pre.at[2]),
        ]

    def kept(self, c, i, b, j):
        turned = self.p.order == "yzx"
        place = lambda u: (j(u), b) if turned else (b, j(u))
        return [lambda u, q=q: self.raw(i, q, *place(u), c) for q in (self.me[0], self.near(0, 3), self.near(0, 1))]

    def own_sum(self, c, i, z):
        first = z * self.p.step
        place = lambda u: first + u
        srcs = self.kept(c, i, self.me[1], place)
        return [*srcs, *(lambda u, ref=ref: ref.at[c, i, place(u)] for ref in (self.LB, self.RB))]

    def stage(self, s, c):
        p = self.p
        if s == 0:
            copies, local = self.sum_copies(0, c), self.local(c)
            for kind in (0, 1, 2, 3):
                copies[kind].start()
            for one in local:
                one.start()
        elif s == 1:
            arrivals, copies, local = self.sum_arrivals(0, c), self.sum_copies(0, c), self.local(c)
            half, opposite = lax.rem(c, 2), self.near(0, 2)
            for h in (0, 1):
                local[h].wait()
                arrivals[h].wait_recv()
                at = lambda u: (lax.div(u, p.units), lax.rem(u, p.units))
                dst = lambda u: self.raw(h, opposite, *at(u), c)
                self.add(4 * p.units, dst, dst, lambda u: self.CB.at[(half, h, *at(u))])
                copies[4 + h].start()
        elif s == 2:
            arrivals, copies = self.sum_arrivals(0, c), self.sum_copies(1, c)
            for kind in (2, 3, 4, 5):
                arrivals[kind].wait_recv()
            self.local(c)[2].wait()
            right, left, opposite = self.near(1, 1), self.near(1, 3), self.near(1, 2)
            for kind, (i, b) in enumerate(((0, opposite), (1, opposite), (1, right), (0, left))):
                srcs = self.kept(c, i, b, lambda u: u)
                self.add(p.units, srcs[1], *srcs)
                copies[kind].start()
        elif s == 3:
            copies = self.sum_copies(1, c)
            for h, b in ((0, self.near(1, 1)), (1, self.near(1, 3))):
                copies[h].wait_recv()
                dst = lambda u: self.SB.at[c, h, u]
                self.add(p.units, dst, *self.kept(c, h, b, lambda u: u), dst)
                copies[4 + h].start()
            self.credit(1, c)
        elif s == 4:
            before, copies = self.sum_copies(1, c), self.sum_copies(2, c)
            for kind in (2, 3, 4, 5):
                before[kind].wait_recv()
            right, left, opposite = self.near(2, 1), self.near(2, 3), self.near(2, 2)
            for kind, (i, z) in enumerate(((0, opposite), (1, opposite), (1, right), (0, left))):
                self.add(p.window, lambda u: self.XC.at[c, kind, u], *self.own_sum(c, i, z))
                copies[kind].start()
        elif s == 5:
            copies = self.sum_copies(2, c)
            for h, z in ((0, self.near(2, 1)), (1, self.near(2, 3))):
                copies[h].wait_recv()
                dst = lambda u: self.SC.at[c, h, u]
                self.add(p.window, dst, *self.own_sum(c, h, z), dst)
                copies[4 + h].start()
            if not p.down:
                self.credit(2, c)
        elif s == 6:
            before, copies = self.sum_copies(2, c), self.gather_copies(2, c)
            for kind in (2, 3, 4, 5):
                before[kind].wait_recv()

            @pl.when(c == 0)
            def _():
                for one in self.preload():
                    one.wait()
                if p.down:
                    self.moments(True)

            self.update(c)
            if not p.down:
                pl.semaphore_wait(self.free.at[c, 2], 2)
            copies[0].start()
            copies[1].start()
            for one in self.sent_from_out(c):
                one.wait_send()
            self.credit(0, c)
            if p.down:

                @pl.when(c == p.chunks - 1)
                def _():
                    self.moments(False)
        elif s in (7, 9, 11):
            phase = {7: 2, 9: 1, 11: 0}[s]
            arrivals, copies = self.gather_arrivals(phase, c), self.gather_copies(phase, c)
            arrivals[0].wait_recv()
            copies[2].start()
            arrivals[1].wait_recv()
            copies[3].start()
        elif s in (8, 10):
            phase = {8: 1, 10: 0}[s]
            arrivals, copies = self.gather_arrivals(phase + 1, c), self.gather_copies(phase, c)
            arrivals[2].wait_recv()
            arrivals[3].wait_recv()
            if s == 8 and p.down:
                self.merge(c)
            pl.semaphore_wait(self.free.at[c, phase], 2)
            copies[0].start()
            copies[1].start()

    def sent_from_out(self, c):
        return [*self.sum_copies(0, c)[4:], *self.sum_copies(1, c)[:4]]

    def update(self, c):
        p = self.p
        cols = self.cols(c)
        z = self.me[2]
        for i in (0, 1):
            srcs = [*self.own_sum(c, i, z), lambda u, i=i: self.LC.at[c, i, u], lambda u, i=i: self.RC.at[c, i, u]]

            @pl.loop(0, p.window)
            def _(u):
                total = srcs[0](u)[...].astype(F32)
                for s in srcs[1:]:
                    total = total + s(u)[...].astype(F32)
                g = total.astype(BF16).astype(F32)
                if p.down:
                    rows = pl.ds(pl.multiple_of(u * p.rows, p.rows), p.rows)
                    mr, vr = self.mb.at[i, rows, cols], self.vb.at[i, rows, cols]
                else:
                    mr, vr = self.mout.at[i, :, cols], self.vout.at[i, :, cols]
                m = 0.9 * mr[...] + 0.1 * g
                v = 0.95 * vr[...] + 0.05 * g * g
                w = self.wb[i, u, :, cols].astype(F32)
                w = (w - 0.02 * (m * lax.rsqrt(v + 1e-8) + 0.1 * w)).astype(BF16)
                mr[...] = m
                vr[...] = v
                if p.down:
                    self.WN[c, z, i, u] = w
                else:
                    self.part(self.out, i, c, *self.me)[...] = w

    def moments(self, into):
        first = 2 * self.at["z"]

        @pl.loop(0, 50)
        def _(r):
            for whole, held in ((self.mout, self.mb), (self.vout, self.vb)):
                for i in (0, 1):
                    if into:
                        held[i, pl.ds(first + r, 1), :] = whole[r, pl.ds(i, 1), :]
                    else:
                        whole[r, pl.ds(i, 1), :] = held[i, pl.ds(first + r, 1), :]

    def merge(self, c):
        p = self.p
        row = lax.broadcasted_iota(jnp.int32, (p.rows, p.width), 0)
        a, b = self.me[:2]
        for i in (0, 1):
            for z in range(4):
                low = 0 if z == 0 else 1
                high = 7 if z == 3 else 6

                @pl.loop(low, high)
                def _(u):
                    self.raw(i, a, b, 6 * z + u, c)[...] = self.WN[c, z, i, u]

                if z:
                    below = self.WN[c, z - 1, i, 6].astype(F32)
                    above = self.WN[c, z, i, 0].astype(F32)
                    self.raw(i, a, b, 6 * z, c)[...] = jnp.where(row < 2 * z, below, above).astype(BF16)

    def finish(self, c):
        for arrival in self.gather_arrivals(0, c)[2:]:
            arrival.wait_recv()
        waited = self.sum_copies(0, c)[:4] + self.sum_copies(1, c)[4:] + self.sum_copies(2, c)
        for phase in range(3):
            waited += self.gather_copies(phase, c)
        for copy in waited:
            copy.wait_send()


def kernel(*refs):
    ins, outs, rest = refs[:12], refs[12:21], refs[21:]
    i = lax.axis_index("dp")
    at = {"x": lax.div(i, 16), "y": lax.rem(lax.div(i, 4), 4), "z": lax.rem(i, 4)}
    runs = []
    for n, p in enumerate(PARTS):
        buffers = dict(zip(SCRATCH, rest[n * len(SCRATCH) : (n + 1) * len(SCRATCH)]))
        runs.append(Run(p, at, *ins[n::3], *outs[n::3], **buffers))
    last = max(p.chunks for p in PARTS) + STAGES - 1

    barrier = pltpu.get_barrier_semaphore()
    for phase in range(3):
        for offset in (1, 3):
            pl.semaphore_signal(barrier, inc=1, device_id=runs[0].device(phase, offset), device_id_type=MESH)
    pl.semaphore_wait(barrier, 6)
    for run in runs:
        for one in run.preload():
            one.start()

    @pl.loop(0, last)
    def _(t):
        for s in range(STAGES):
            for run in runs:

                @pl.when((t >= s) & (t - s < run.p.chunks))
                def _(run=run, s=s):
                    run.stage(s, t - s)

    for run in runs:

        @pl.loop(0, run.p.chunks)
        def _(c, run=run):
            run.finish(c)


def sum_step_gather(terms, weights, m, v):
    shapes = [(2, 4, 4, 4, 16, 3200)] * 2 + [(2, 4, 4, 25, 8, 1024)]
    moments = [a.shape for a in m]
    args = [a.reshape(s) for group in (terms, weights) for a, s in zip(group, shapes, strict=True)] + [*m, *v]
    held = [one for p in PARTS for one in (lambda made: [made[name] for name in SCRATCH])(scratch(p))]
    hbm = pl.BlockSpec(memory_space=pl.ANY)
    vmem = pl.BlockSpec(memory_space=pltpu.VMEM)
    made = pl.pallas_call(
        kernel,
        name="sum_step_gather",
        out_shape=[pltpu.VMEM(s, BF16) for s in shapes] + [pltpu.VMEM(s, F32) for s in moments * 2],
        in_specs=[hbm] * 12,
        out_specs=[vmem] * 9,
        scratch_shapes=held,
        compiler_params=pltpu.CompilerParams(collective_id=0, has_side_effects=True, vmem_limit_bytes=VMEM_LIMIT),
    )(*args)
    return pl.pallas_call(
        write_out,
        name="write_out",
        out_shape=[jax.ShapeDtypeStruct(a.shape, a.dtype) for a in made],
        in_specs=[vmem] * 9,
        out_specs=[hbm] * 9,
        scratch_shapes=[pltpu.SemaphoreType.DMA((9, 2))],
        compiler_params=pltpu.CompilerParams(vmem_limit_bytes=VMEM_LIMIT),
    )(*(pltpu.with_memory_space_constraint(a, pltpu.VMEM) for a in made))


def write_out(*refs):
    ins, outs, sems = refs[:9], refs[9:18], refs[18]
    copies = []
    for n, (src, dst) in enumerate(zip(ins, outs, strict=True)):
        if n < 3:
            copies += [pltpu.make_async_copy(src.at[i], dst.at[i], sems.at[n, i]) for i in (0, 1)]
        else:
            copies.append(pltpu.make_async_copy(src, dst, sems.at[n, 0]))
    for one in copies:
        one.start()
    for one in copies:
        one.wait()


def solution(mesh):
    def step(*arrays):
        terms, weights, m, v = (arrays[i : i + 3] for i in (0, 3, 6, 9))
        turn = lambda a: [*a[:2], a[2].transpose(1, 0, 2)]
        out = sum_step_gather(terms, weights, turn(m), turn(v))
        new = [a.reshape(w.shape) for a, w in zip(out[:3], weights, strict=True)]
        return (*new, *turn(out[3:6]), *turn(out[6:9]))

    all_of, cut = P(None, None, None), P(None, "dp", None)
    return jax.shard_map(
        step,
        mesh=mesh,
        in_specs=(P(("rep", "dp"), None, None, None),) * 3 + (all_of,) * 3 + (cut,) * 6,
        out_specs=(P("rep", None, None),) * 3 + (P("rep", "dp", None),) * 6,
        check_vma=False,
    )
```

time: 335 us -> 311 us (0.928)
  local copies, waits for them, and re-layouts: 32.4 us -> 0 us
  Pallas kernels: 296 us -> 310 us
  other arithmetic: 5.56 us -> 0 us
    unnamed x19 -> x0, local copies, waits for them, and re-layouts: 30.5 us -> none
    pallas_call x1 -> x2, Pallas kernels: 296 us -> 310 us  [the longest x1 297 us: sum_step_gather(): pl.pallas_call(kernel, name='sum_step_gather', out_shape=[pltpu.VMEM(s, B...]
    add x2 -> x0, other arithmetic: 5.56 us -> none  [step(): new_v = [0.95 * a + 0.05 * b * b for a, b in zip(v, g, strict=True)]]
where the time goes in v2:
time: 311 us
  Pallas kernels  310 us (100%)
    pallas_call x1, Pallas kernels, sum_step_gather(): pl.pallas_call(kernel, name='sum_step_gather', out_shape=[pltpu.VMEM(s, B...  297 us
    pallas_call x1, Pallas kernels, sum_step_gather(): pl.pallas_call(write_out, name='write_out', out_shape=[jax.ShapeDtypeStru...  13.5 us

profile of v2, /device:TPU:0, one launch (start us, length us, event | category | flops | bytes accessed | tf_op | source)
XLA Modules:
  0.0 310.8 jit_solution(8686601856355562376)
XLA Ops:
  0.6 296.6 %sum_step_gather.1 = (bf16[2,4,4,4,16,3200]{5,4,3,2,1,0:T(8,128)(2,1)S(1)}, bf16[2,4,4,4,16,3200]{5,4,3,2,1,0:T(8,128)(2,1)S(1)}, bf16[2,4,4,25,8,1024]{5,4,3,2,...) custom-call(bf16[2,4,4,4,16,3200]{5,4,3,2,1,0:T(8,128)(2,1)} %bitcas, ...), custom_call_target="tpu_custom_call" | custom-call | tf_op jit(solution)/shard_map/sum_step_gather/pallas_call | solution.py:409
  297.3 13.5 %write_out.1 = (bf16[2,4,4,4,16,3200]{5,4,3,2,1,0:T(8,128)(2,1)}, bf16[2,4,4,4,16,3200]{5,4,3,2,1,0:T(8,128)(2,1)}, bf16[2,4,4,25,8,1024]{5,4,3,2,1,0:T(8,128)(2...) custom-call(bf16[2,4,4,4,16,3200]{5,4,3,2,1,0:T(8,128)(2,1)S(1)} %ge, ...), custom_call_target="tpu_custom_call" | custom-call | tf_op jit(solution)/shard_map/write_out/pallas_call | solution.py:418

commit v3 on v2

--- a/solution.py
+++ b/solution.py
@@ -10,35 +10,44 @@
 F32, BF16 = jnp.float32, jnp.bfloat16
 MESH = pl.DeviceIdType.MESH
 STAGES = 12
+GATE_CUTS = ((1, 1152), (2, 1024))
+DOWN_CUTS = ((2, 384), (1, 256))
+DOWN_BLOCK = 5
 VMEM_LIMIT = 24 << 20
 
 
 class Part:
-    def __init__(self, order, chunks, width, units, window, step, rows):
-        self.order, self.chunks, self.width = order, chunks, width
-        self.units, self.window, self.step, self.rows = units, window, step, rows
+    def __init__(self, order, cuts, units, window, step, rows, block):
+        self.order, self.units, self.window, self.step, self.rows, self.block = order, units, window, step, rows, block
         self.down = window > 1
+        self.chunks = sum(count for count, _ in cuts)
+        self.widest = max(width for _, width in cuts)
+        self.columns = sum(count * width for count, width in cuts)
+        self.groups, chunk, column = [], 0, 0
+        for count, width in cuts:
+            self.groups.append((chunk, chunk + count, column, width))
+            chunk, column = chunk + count, column + count * width
 
 
 PARTS = (
-    Part("yzx", 5, 640, 4, 1, 1, 16),
-    Part("zxy", 5, 640, 4, 1, 1, 16),
-    Part("xyz", 4, 256, 25, 7, 6, 8),
+    Part("yzx", GATE_CUTS, 4, 1, 1, 16, 4),
+    Part("zxy", GATE_CUTS, 4, 1, 1, 16, 4),
+    Part("xyz", DOWN_CUTS, 25, 7, 6, 8, DOWN_BLOCK),
 )
 SCRATCH = ("CB", "SB", "LB", "RB", "SC", "LC", "RC", "XC", "WN", "mb", "vb", "wb", "send", "recv", "gsend", "grecv", "loc", "pre", "free")
 
 
 def scratch(p):
-    k, u, w, r, n = p.chunks, p.units, p.width, p.rows, p.window
+    k, u, w, r, n = p.chunks, p.units, p.widest, p.rows, p.window
     group = lambda *lead: pltpu.VMEM((*lead, u, r, w), BF16)
     win = lambda *lead: pltpu.VMEM((*lead, n, r, w), BF16)
-    moment = pltpu.VMEM((2, n * r, k * w) if p.down else (8, 128), F32)
+    moment = pltpu.VMEM((2, n * r, p.columns) if p.down else (8, 128), F32)
     dma = pltpu.SemaphoreType.DMA
     return {
-        "CB": group(2, 2, 4), "SB": group(k, 2), "LB": group(k, 2), "RB": group(k, 2),
-        "SC": win(k, 2), "LC": win(k, 2), "RC": win(k, 2), "XC": win(k, 4),
+        "CB": group(2, 2, 4), "SB": group(k, 2, 2), "LB": group(k, 2), "RB": group(k, 2),
+        "SC": win(k, 2, 2), "LC": win(k, 2), "RC": win(k, 2), "XC": win(k, 2),
         "WN": win(k, 4, 2) if p.down else pltpu.VMEM((16, 128), BF16),
-        "mb": moment, "vb": moment, "wb": pltpu.VMEM((2, n, r, k * w), BF16),
+        "mb": moment, "vb": moment, "wb": pltpu.VMEM((2, n, r, p.columns), BF16),
         "send": dma((k, 3, 6)), "recv": dma((k, 3, 6)), "gsend": dma((k, 3, 4)), "grecv": dma((k, 3, 4)),
         "loc": dma((k, 3)), "pre": dma((3,)), "free": pltpu.SemaphoreType.REGULAR((k, 3)),
     }
@@ -78,8 +87,17 @@
     def near(self, phase, offset):
         return lax.rem(self.me[phase] + offset, 4)
 
+    def use(self, group):
+        self.first, _, self.column, self.width = group
+        return self
+
     def cols(self, c):
-        return pl.ds(pl.multiple_of(c * self.p.width, 128), self.p.width)
+        return pl.ds(pl.multiple_of(self.column + (c - self.first) * self.width, 128), self.width)
+
+    def cut(self, ref, *where):
+        if self.width == self.p.widest:
+            return ref.at[where]
+        return ref.at[(*where, *[slice(None)] * (len(ref.shape) - len(where) - 1), pl.ds(0, self.width))]
 
     def part(self, ref, layer, c, a=None, b=None, z=None):
         of = dict(zip(self.p.order, (a, b, z)))
@@ -108,12 +126,16 @@
             pl.semaphore_signal(self.free.at[c, phase], inc=1, device_id=self.device(phase, offset), device_id_type=MESH)
 
     def add(self, n, dst, *srcs):
-        @pl.loop(0, n)
-        def _(j):
+        def one(j):
             total = srcs[0](j)[...].astype(F32)
             for s in srcs[1:]:
                 total = total + s(j)[...].astype(F32)
             dst(j)[...] = total.astype(BF16)
+
+        if n == 1:
+            one(0)
+        else:
+            pl.loop(0, n)(one)
 
     def sum_copies(self, phase, c):
         right, left, opposite = self.near(phase, 1), self.near(phase, 3), self.near(phase, 2)
@@ -126,12 +148,12 @@
         else:
             s, l, r = ((self.SB, self.LB, self.RB), (self.SC, self.LC, self.RC))[phase - 1]
             if phase == 1:
-                src = [self.part(self.out, i, c, self.near(0, 3), b) for i, b in kinds]
+                src = [self.part(self.out, i, c, self.near(0, 3), opposite) for i in (0, 1)]
             else:
-                src = [self.XC.at[c, i] for i in range(4)]
-            src += [s.at[c, 0], s.at[c, 1]]
-            dst = [s.at[c, 0], s.at[c, 1], l.at[c, 1], r.at[c, 0], l.at[c, 0], r.at[c, 1]]
-        return [self.to(src[kind], dst[kind], (self.send, self.recv), phase, kind, c) for kind in range(6)]
+                src = [self.cut(self.XC, c, i) for i in (0, 1)]
+            src += [self.cut(s, c, 0), self.cut(s, c, 1)]
+            dst = [self.cut(s, c, 0, 0), self.cut(s, c, 1, 1), self.cut(l, c), self.cut(r, c)]
+        return [self.to(one, there, (self.send, self.recv), phase, kind, c) for kind, (one, there) in enumerate(zip(src, dst, strict=True))]
 
     def sum_arrivals(self, phase, c):
         if phase:
@@ -145,7 +167,7 @@
         a, b, z = self.me
         if phase == 2:
             z = self.near(2, offset)
-            return self.WN.at[c, z, layer] if self.p.down else self.part(self.out, layer, c, a, b, z)
+            return self.cut(self.WN, c, z, layer) if self.p.down else self.part(self.out, layer, c, a, b, z)
         if phase == 1:
             return self.part(self.out, layer, c, a, self.near(1, offset))
         return self.part(self.out, layer, c, self.near(0, offset))
@@ -167,8 +189,8 @@
         copy = lambda *refs: Later(lambda: pltpu.make_async_copy(*refs))
         half, mine, both = lax.rem(c, 2), self.me[0], pl.ds(0, 2)
         return [
-            copy(self.part(self.gh, 0, c, self.near(0, 1)), self.CB.at[half, 0], self.loc.at[c, 0]),
-            copy(self.part(self.gh, 1, c, self.near(0, 3)), self.CB.at[half, 1], self.loc.at[c, 1]),
+            copy(self.part(self.gh, 0, c, self.near(0, 1)), self.cut(self.CB, half, 0), self.loc.at[c, 0]),
+            copy(self.part(self.gh, 1, c, self.near(0, 3)), self.cut(self.CB, half, 1), self.loc.at[c, 1]),
             copy(self.part(self.gh, both, c, mine), self.part(self.out, both, c, mine), self.loc.at[c, 2]),
         ]
 
@@ -191,13 +213,13 @@
         return [lambda u, q=q: self.raw(i, q, *place(u), c) for q in (self.me[0], self.near(0, 3), self.near(0, 1))]
 
     def own_sum(self, c, i, z):
-        first = z * self.p.step
-        place = lambda u: first + u
+        place = lambda u: pl.ds(z * self.p.step, self.p.window)
         srcs = self.kept(c, i, self.me[1], place)
-        return [*srcs, *(lambda u, ref=ref: ref.at[c, i, place(u)] for ref in (self.LB, self.RB))]
+        return [*srcs, *(lambda u, ref=ref: self.cut(ref, c, i, place(u)) for ref in (self.LB, self.RB))]
 
     def stage(self, s, c):
         p = self.p
+        block = lambda u: pl.ds(u * p.block, p.block)
         if s == 0:
             copies, local = self.sum_copies(0, c), self.local(c)
             for kind in (0, 1, 2, 3):
@@ -206,13 +228,13 @@
                 one.start()
         elif s == 1:
             arrivals, copies, local = self.sum_arrivals(0, c), self.sum_copies(0, c), self.local(c)
-            half, opposite = lax.rem(c, 2), self.near(0, 2)
+            half, opposite, blocks = lax.rem(c, 2), self.near(0, 2), p.units // p.block
             for h in (0, 1):
                 local[h].wait()
                 arrivals[h].wait_recv()
-                at = lambda u: (lax.div(u, p.units), lax.rem(u, p.units))
+                at = lambda u: (lax.div(u, blocks), pl.ds(lax.rem(u, blocks) * p.block, p.block))
                 dst = lambda u: self.raw(h, opposite, *at(u), c)
-                self.add(4 * p.units, dst, dst, lambda u: self.CB.at[(half, h, *at(u))])
+                self.add(4 * blocks, dst, dst, lambda u: self.cut(self.CB, half, h, *at(u)))
                 copies[4 + h].start()
         elif s == 2:
             arrivals, copies = self.sum_arrivals(0, c), self.sum_copies(1, c)
@@ -220,38 +242,43 @@
                 arrivals[kind].wait_recv()
             self.local(c)[2].wait()
             right, left, opposite = self.near(1, 1), self.near(1, 3), self.near(1, 2)
-            for kind, (i, b) in enumerate(((0, opposite), (1, opposite), (1, right), (0, left))):
-                srcs = self.kept(c, i, b, lambda u: u)
-                self.add(p.units, srcs[1], *srcs)
-                copies[kind].start()
+            blocks = p.units // p.block
+            for i in (0, 1):
+                srcs = self.kept(c, i, opposite, block)
+                self.add(blocks, srcs[1], *srcs)
+                copies[i].start()
+            for way, i, b in ((0, 1, right), (1, 0, left)):
+                self.add(blocks, lambda u: self.cut(self.SB, c, way, i, block(u)), *self.kept(c, i, b, block))
         elif s == 3:
             copies = self.sum_copies(1, c)
             for h, b in ((0, self.near(1, 1)), (1, self.near(1, 3))):
                 copies[h].wait_recv()
-                dst = lambda u: self.SB.at[c, h, u]
-                self.add(p.units, dst, *self.kept(c, h, b, lambda u: u), dst)
-                copies[4 + h].start()
+                dst = lambda u: self.cut(self.SB, c, h, h, block(u))
+                self.add(p.units // p.block, dst, *self.kept(c, h, b, block), dst)
+                copies[2 + h].start()
             self.credit(1, c)
         elif s == 4:
             before, copies = self.sum_copies(1, c), self.sum_copies(2, c)
-            for kind in (2, 3, 4, 5):
+            for kind in (2, 3):
                 before[kind].wait_recv()
             right, left, opposite = self.near(2, 1), self.near(2, 3), self.near(2, 2)
-            for kind, (i, z) in enumerate(((0, opposite), (1, opposite), (1, right), (0, left))):
-                self.add(p.window, lambda u: self.XC.at[c, kind, u], *self.own_sum(c, i, z))
-                copies[kind].start()
+            for i in (0, 1):
+                self.add(1, lambda u: self.cut(self.XC, c, i), *self.own_sum(c, i, opposite))
+                copies[i].start()
+            for way, i, z in ((0, 1, right), (1, 0, left)):
+                self.add(1, lambda u: self.cut(self.SC, c, way, i), *self.own_sum(c, i, z))
         elif s == 5:
             copies = self.sum_copies(2, c)
             for h, z in ((0, self.near(2, 1)), (1, self.near(2, 3))):
                 copies[h].wait_recv()
-                dst = lambda u: self.SC.at[c, h, u]
-                self.add(p.window, dst, *self.own_sum(c, h, z), dst)
-                copies[4 + h].start()
+                dst = lambda u: self.cut(self.SC, c, h, h)
+                self.add(1, dst, *self.own_sum(c, h, z), dst)
+                copies[2 + h].start()
             if not p.down:
                 self.credit(2, c)
         elif s == 6:
             before, copies = self.sum_copies(2, c), self.gather_copies(2, c)
-            for kind in (2, 3, 4, 5):
+            for kind in (2, 3):
                 before[kind].wait_recv()
 
             @pl.when(c == 0)
@@ -293,36 +320,29 @@
             copies[1].start()
 
     def sent_from_out(self, c):
-        return [*self.sum_copies(0, c)[4:], *self.sum_copies(1, c)[:4]]
+        return [*self.sum_copies(0, c)[4:], *self.sum_copies(1, c)[:2]]
 
     def update(self, c):
         p = self.p
         cols = self.cols(c)
         z = self.me[2]
         for i in (0, 1):
-            srcs = [*self.own_sum(c, i, z), lambda u, i=i: self.LC.at[c, i, u], lambda u, i=i: self.RC.at[c, i, u]]
-
-            @pl.loop(0, p.window)
-            def _(u):
-                total = srcs[0](u)[...].astype(F32)
-                for s in srcs[1:]:
-                    total = total + s(u)[...].astype(F32)
-                g = total.astype(BF16).astype(F32)
-                if p.down:
-                    rows = pl.ds(pl.multiple_of(u * p.rows, p.rows), p.rows)
-                    mr, vr = self.mb.at[i, rows, cols], self.vb.at[i, rows, cols]
-                else:
-                    mr, vr = self.mout.at[i, :, cols], self.vout.at[i, :, cols]
-                m = 0.9 * mr[...] + 0.1 * g
-                v = 0.95 * vr[...] + 0.05 * g * g
-                w = self.wb[i, u, :, cols].astype(F32)
-                w = (w - 0.02 * (m * lax.rsqrt(v + 1e-8) + 0.1 * w)).astype(BF16)
-                mr[...] = m
-                vr[...] = v
-                if p.down:
-                    self.WN[c, z, i, u] = w
-                else:
-                    self.part(self.out, i, c, *self.me)[...] = w
+            srcs = [*self.own_sum(c, i, z), *(lambda u, ref=ref: self.cut(ref, c, i) for ref in (self.LC, self.RC))]
+            total = srcs[0](0)[...].astype(F32)
+            for s in srcs[1:]:
+                total = total + s(0)[...].astype(F32)
+            g = total.astype(BF16).astype(F32).reshape(p.window * p.rows, self.width)
+            mr, vr = (self.mb, self.vb) if p.down else (self.mout, self.vout)
+            m = 0.9 * mr[i, :, cols] + 0.1 * g
+            v = 0.95 * vr[i, :, cols] + 0.05 * g * g
+            w = self.wb[i, :, :, cols].astype(F32).reshape(p.window * p.rows, self.width)
+            w = (w - 0.02 * (m * lax.rsqrt(v + 1e-8) + 0.1 * w)).reshape(p.window, p.rows, self.width).astype(BF16)
+            mr[i, :, cols] = m
+            vr[i, :, cols] = v
+            if p.down:
+                self.cut(self.WN, c, z, i)[...] = w
+            else:
+                self.part(self.out, i, c, *self.me)[...] = w[0]
 
     def moments(self, into):
         first = 2 * self.at["z"]
@@ -338,26 +358,22 @@
 
     def merge(self, c):
         p = self.p
-        row = lax.broadcasted_iota(jnp.int32, (p.rows, p.width), 0)
+        row = lax.broadcasted_iota(jnp.int32, (p.rows, self.width), 0)
         a, b = self.me[:2]
         for i in (0, 1):
             for z in range(4):
                 low = 0 if z == 0 else 1
                 high = 7 if z == 3 else 6
-
-                @pl.loop(low, high)
-                def _(u):
-                    self.raw(i, a, b, 6 * z + u, c)[...] = self.WN[c, z, i, u]
-
+                self.raw(i, a, b, pl.ds(6 * z + low, high - low), c)[...] = self.cut(self.WN, c, z, i, pl.ds(low, high - low))[...]
                 if z:
-                    below = self.WN[c, z - 1, i, 6].astype(F32)
-                    above = self.WN[c, z, i, 0].astype(F32)
+                    below = self.cut(self.WN, c, z - 1, i, 6)[...].astype(F32)
+                    above = self.cut(self.WN, c, z, i, 0)[...].astype(F32)
                     self.raw(i, a, b, 6 * z, c)[...] = jnp.where(row < 2 * z, below, above).astype(BF16)
 
     def finish(self, c):
         for arrival in self.gather_arrivals(0, c)[2:]:
             arrival.wait_recv()
-        waited = self.sum_copies(0, c)[:4] + self.sum_copies(1, c)[4:] + self.sum_copies(2, c)
+        waited = self.sum_copies(0, c)[:4] + self.sum_copies(1, c)[2:] + self.sum_copies(2, c)
         for phase in range(3):
             waited += self.gather_copies(phase, c)
         for copy in waited:
@@ -387,16 +403,18 @@
     def _(t):
         for s in range(STAGES):
             for run in runs:
-
-                @pl.when((t >= s) & (t - s < run.p.chunks))
-                def _(run=run, s=s):
-                    run.stage(s, t - s)
+                for group in run.p.groups:
+
+                    @pl.when((t - s >= group[0]) & (t - s < group[1]))
+                    def _(run=run, s=s, group=group):
+                        run.use(group).stage(s, t - s)
 
     for run in runs:
-
-        @pl.loop(0, run.p.chunks)
-        def _(c, run=run):
-            run.finish(c)
+        for group in run.p.groups:
+
+            @pl.loop(group[0], group[1])
+            def _(c, run=run, group=group):
+                run.use(group).finish(c)
 
 
 def sum_step_gather(terms, weights, m, v):

time: 311 us -> 307 us (0.987)
  Pallas kernels: 310 us -> 306 us
    pallas_call x1, Pallas kernels: 297 us -> 293 us  [sum_step_gather(): pl.pallas_call(kernel, name='sum_step_gather', out_shape=[pltpu.VMEM(s, B...]
where the time goes in v3:
time: 307 us
  Pallas kernels  306 us (100%)
    pallas_call x1, Pallas kernels, sum_step_gather(): pl.pallas_call(kernel, name='sum_step_gather', out_shape=[pltpu.VMEM(s, B...  293 us
    pallas_call x1, Pallas kernels, sum_step_gather(): pl.pallas_call(write_out, name='write_out', out_shape=[jax.ShapeDtypeStru...  13.5 us

profile of v3, /device:TPU:0, one launch (start us, length us, event | category | flops | bytes accessed | tf_op | source)
XLA Modules:
  0.0 307.1 jit_solution(1206507926857078048)
XLA Ops:
  0.6 292.9 %sum_step_gather.1 = (bf16[2,4,4,4,16,3200]{5,4,3,2,1,0:T(8,128)(2,1)S(1)}, bf16[2,4,4,4,16,3200]{5,4,3,2,1,0:T(8,128)(2,1)S(1)}, bf16[2,4,4,25,8,1024]{5,4,3,2,...) custom-call(bf16[2,4,4,4,16,3200]{5,4,3,2,1,0:T(8,128)(2,1)} %bitcas, ...), custom_call_target="tpu_custom_call" | custom-call | tf_op jit(solution)/shard_map/sum_step_gather/pallas_call | solution.py:427
  293.5 13.5 %write_out.1 = (bf16[2,4,4,4,16,3200]{5,4,3,2,1,0:T(8,128)(2,1)}, bf16[2,4,4,4,16,3200]{5,4,3,2,1,0:T(8,128)(2,1)}, bf16[2,4,4,25,8,1024]{5,4,3,2,1,0:T(8,128)(2...) custom-call(bf16[2,4,4,4,16,3200]{5,4,3,2,1,0:T(8,128)(2,1)S(1)} %ge, ...), custom_call_target="tpu_custom_call" | custom-call | tf_op jit(solution)/shard_map/write_out/pallas_call | solution.py:436

commit v4 on v3

--- a/solution.py
+++ b/solution.py
@@ -308,6 +308,8 @@
             copies[2].start()
             arrivals[1].wait_recv()
             copies[3].start()
+            if s == 11:
+                self.sent(c)
         elif s in (8, 10):
             phase = {8: 1, 10: 0}[s]
             arrivals, copies = self.gather_arrivals(phase + 1, c), self.gather_copies(phase, c)
@@ -370,14 +372,16 @@
                     above = self.cut(self.WN, c, z, i, 0)[...].astype(F32)
                     self.raw(i, a, b, 6 * z, c)[...] = jnp.where(row < 2 * z, below, above).astype(BF16)
 
+    def sent(self, c):
+        waited = self.sum_copies(0, c)[:4] + self.sum_copies(1, c)[2:] + self.sum_copies(2, c)
+        for copy in (*waited, *self.gather_copies(2, c), *self.gather_copies(1, c)):
+            copy.wait_send()
+
     def finish(self, c):
+        for copy in self.gather_copies(0, c):
+            copy.wait_send()
         for arrival in self.gather_arrivals(0, c)[2:]:
             arrival.wait_recv()
-        waited = self.sum_copies(0, c)[:4] + self.sum_copies(1, c)[2:] + self.sum_copies(2, c)
-        for phase in range(3):
-            waited += self.gather_copies(phase, c)
-        for copy in waited:
-            copy.wait_send()
 
 
 def kernel(*refs):
@@ -394,10 +398,10 @@
     for phase in range(3):
         for offset in (1, 3):
             pl.semaphore_signal(barrier, inc=1, device_id=runs[0].device(phase, offset), device_id_type=MESH)
-    pl.semaphore_wait(barrier, 6)
     for run in runs:
         for one in run.preload():
             one.start()
+    pl.semaphore_wait(barrier, 6)
 
     @pl.loop(0, last)
     def _(t):

time: 307 us -> 307 us (level)
  no operation moved by 1% of the time
where the time goes in v4:
time: 307 us
  Pallas kernels  306 us (100%)
    pallas_call x1, Pallas kernels, sum_step_gather(): pl.pallas_call(kernel, name='sum_step_gather', out_shape=[pltpu.VMEM(s, B...  293 us
    pallas_call x1, Pallas kernels, sum_step_gather(): pl.pallas_call(write_out, name='write_out', out_shape=[jax.ShapeDtypeStru...  13.5 us

profile of v4, /device:TPU:0, one launch (start us, length us, event | category | flops | bytes accessed | tf_op | source)
XLA Modules:
  0.0 306.9 jit_solution(9798642058863148785)
XLA Ops:
  0.6 292.7 %sum_step_gather.1 = (bf16[2,4,4,4,16,3200]{5,4,3,2,1,0:T(8,128)(2,1)S(1)}, bf16[2,4,4,4,16,3200]{5,4,3,2,1,0:T(8,128)(2,1)S(1)}, bf16[2,4,4,25,8,1024]{5,4,3,2,...) custom-call(bf16[2,4,4,4,16,3200]{5,4,3,2,1,0:T(8,128)(2,1)} %bitcas, ...), custom_call_target="tpu_custom_call" | custom-call | tf_op jit(solution)/shard_map/sum_step_gather/pallas_call | solution.py:431
  293.3 13.5 %write_out.1 = (bf16[2,4,4,4,16,3200]{5,4,3,2,1,0:T(8,128)(2,1)}, bf16[2,4,4,4,16,3200]{5,4,3,2,1,0:T(8,128)(2,1)}, bf16[2,4,4,25,8,1024]{5,4,3,2,1,0:T(8,128)(2...) custom-call(bf16[2,4,4,4,16,3200]{5,4,3,2,1,0:T(8,128)(2,1)S(1)} %ge, ...), custom_call_target="tpu_custom_call" | custom-call | tf_op jit(solution)/shard_map/write_out/pallas_call | solution.py:440
